TPU v7x, 32 devices: a whole 2x2x4 slice. The times are simulated.
32 devices in a mesh: dp: 16 (over z, y, x), tensor: 2 (over core).
Axes of the slice: x: 2, y: 2, z: 4, core: 2. Of those that a mesh axis runs over, the one named last changes fastest.
Arguments:
- vis_rows: bfloat16 [8, 128, 2, 3200], P(None, 'dp', None, 'tensor'), may hold values from -6 to 6
- ln_gain: float32 [2, 3200], replicated, may hold values from 0.25 to 1.75
- ln_bias: float32 [2, 3200], replicated, may hold values from -3 to 3
- proj_weight: bfloat16 [3200, 2, 8192], P('dp', None, 'tensor'), may hold values from -0.078125 to 0.078125
- text_rows: bfloat16 [16, 384, 8192], P('dp', None, 'tensor'), may hold values from -8 to 8
- attn_gain: float32 [8192], replicated, may hold values from 0.25 to 1.75
- w_query: bfloat16 [8192, 4096], P('dp', 'tensor'), may hold values from -0.088388348 to 0.088388348
- key_value_weight: bfloat16 [8192, 2, 1024], P('dp', None, 'tensor'), may hold values from -0.088388348 to 0.088388348
- tile_counts: int32 [16], replicated, may hold values from 1 to 16, 128 in all
- image_offsets: int32 [16], P('dp'), may hold values from 0 to 256
Outputs:
- attn_context: bfloat16 [16, 384, 4096], P('dp', None, 'tensor')
Inputs may be any that keep to these rules, and one draw needn't show every extreme that they name: tile_counts counts all 128 tiles, and its largest entry is exactly 16.
All inputs are finite; a program needn't handle non-finite values.
Results may differ from a plain program's by a relative error of at most 0.0074.
Values may be sent and summed in bfloat16 or wider, within the bound.
A program may use at most 128 MiB of HBM per device.

v0:
```python
import jax
import jax.numpy as jnp
from jax import lax
from jax.sharding import PartitionSpec as P

QUERY_HEADS = 32
KEY_VALUE_HEADS = 8
HEAD_WIDTH = 128


vision_epsilon = 1e-06
decoder_epsilon = 1e-05
rope_base = 500000.0


def apply_rotary(value_rows, position_indices):
    half_width = value_rows.shape[-1] // 2
    exponents = jnp.arange(half_width, dtype=jnp.float32) * (2.0 / value_rows.shape[-1])
    frequency = rope_base ** (-exponents)
    angles = position_indices.astype(jnp.float32)[:, None] * frequency[None, :]
    cosine = jnp.cos(angles)[:, None, :]
    sine = jnp.sin(angles)[:, None, :]
    first_half = value_rows[..., :half_width]
    second_half = value_rows[..., half_width:]
    return jnp.concatenate(
        [first_half * cosine - second_half * sine, second_half * cosine + first_half * sine],
        axis=-1,
    )


def layer_norm(value_rows, gain, bias_values):
    average = jnp.mean(value_rows, axis=(-2, -1), keepdims=True)
    centered = value_rows - average
    variance = jnp.mean(centered * centered, axis=(-2, -1), keepdims=True)
    return centered * lax.rsqrt(variance + vision_epsilon) * gain + bias_values


def attend(query_full, key_value_complete):
    seq_len = query_full.shape[0]
    query_group_count = QUERY_HEADS // KEY_VALUE_HEADS
    local_kv = key_value_complete.shape[2] // HEAD_WIDTH
    local_query = query_full.shape[1] // HEAD_WIDTH
    position_indices = jnp.arange(seq_len, dtype=jnp.int32)
    query_rows = apply_rotary(
        query_full.reshape(seq_len, local_query, HEAD_WIDTH), position_indices
    ).astype(jnp.bfloat16)
    query_rows = query_rows.reshape(seq_len, local_kv, query_group_count, HEAD_WIDTH)
    key_rows = apply_rotary(
        key_value_complete[:, 0].reshape(seq_len, local_kv, HEAD_WIDTH), position_indices
    ).astype(jnp.bfloat16)
    value_rows = (
        key_value_complete[:, 1].reshape(seq_len, local_kv, HEAD_WIDTH).astype(jnp.bfloat16)
    )
    scores = jnp.einsum(
        "pgjd,kgd->gjpk", query_rows, key_rows, preferred_element_type=jnp.float32
    ) * HEAD_WIDTH ** (-0.5)
    causal = position_indices[:, None] >= position_indices[None, :]
    scores = jnp.where(causal[None, None], scores, -1e30)
    row_max = jnp.max(scores, axis=-1, keepdims=True)
    exponentials = jnp.exp(scores - row_max)
    weights = (exponentials / jnp.sum(exponentials, axis=-1, keepdims=True)).astype(jnp.bfloat16)
    context = jnp.einsum("gjpk,kgd->pgjd", weights, value_rows, preferred_element_type=jnp.float32)
    return context.astype(jnp.bfloat16).reshape(seq_len, local_query * HEAD_WIDTH)


def per_device(
    vis_rows,
    ln_gain,
    ln_bias,
    proj_weight,
    text_rows,
    attn_gain,
    w_query,
    key_value_weight,
    tile_counts,
    image_offsets,
):
    data_count = lax.axis_size("dp")
    data_index = lax.axis_index("dp")
    tile_rows, tile_tok, merge_count, part_width = vis_rows.shape
    vision_width = ln_gain.shape[1]
    part_model = proj_weight.shape[2]
    token_count = tile_rows * tile_tok
    proj_whole, query_whole, keyval_whole = (
        lax.all_gather(proj_weight, "dp", axis=0, tiled=True),
        lax.all_gather(w_query, "dp", axis=0, tiled=True),
        lax.all_gather(key_value_weight, "dp", axis=0, tiled=True),
    )
    max_tiles = 2 * tile_rows
    slot_count = (max_tiles + data_count - 1) // data_count
    tile_ends = jnp.cumsum(tile_counts)
    tile_firsts = tile_ends - tile_counts
    sample_ids = jnp.arange(data_count, dtype=jnp.int32)
    tiles_here = jnp.arange(tile_rows, dtype=jnp.int32) * data_count + data_index
    owners = jnp.sum((tile_ends[None, :] <= tiles_here[:, None]).astype(jnp.int32), axis=1)
    owner_first = jnp.sum(
        jnp.where(sample_ids[None, :] == owners[:, None], tile_firsts[None, :], 0), axis=1
    )
    slots = (tiles_here - owner_first) // data_count
    is_mine = sample_ids == data_index
    my_first = jnp.sum(jnp.where(is_mine, tile_firsts, 0))
    my_count = jnp.sum(jnp.where(is_mine, tile_counts, 0))
    tile_order = jnp.arange(max_tiles, dtype=jnp.int32)
    sources = (my_first + tile_order) % data_count
    slot_index = tile_order // data_count
    image_span = max_tiles * tile_tok
    whole = lax.all_gather(vis_rows, "tensor", axis=3, tiled=True)
    merged = whole.reshape(token_count, merge_count, vision_width).astype(jnp.float32)
    normed_vis = layer_norm(merged, ln_gain, ln_bias).astype(jnp.bfloat16)
    image_cols = (
        jnp.einsum("rmf,fmo->ro", normed_vis, proj_whole, preferred_element_type=jnp.float32)
        .astype(jnp.bfloat16)
        .reshape(tile_rows, tile_tok, part_model)
    )
    empty_slots = jnp.zeros((data_count, slot_count) + image_cols.shape[1:], jnp.bfloat16)
    received = lax.all_to_all(
        empty_slots.at[owners, slots].set(image_cols), "dp", split_axis=0, concat_axis=0, tiled=True
    )
    arrived = received[sources, slot_index]
    arrived = arrived.reshape(image_span, part_model)
    start_row = image_offsets[0]
    sequence = text_rows[0]
    current = lax.dynamic_slice_in_dim(sequence, start_row, image_span, 0)
    is_image = jnp.repeat(tile_order < my_count, tile_tok)[:, None]
    combined = jnp.where(is_image, arrived, current)
    sequence = lax.dynamic_update_slice_in_dim(sequence, combined, start_row, 0)
    gathered = lax.all_gather(sequence, "tensor", axis=1, tiled=True)
    seq_float = gathered.astype(jnp.float32)
    mean_square = jnp.mean(seq_float * seq_float, axis=-1, keepdims=True)
    normalized_sequence = (seq_float * lax.rsqrt(mean_square + decoder_epsilon) * attn_gain).astype(
        jnp.bfloat16
    )
    seq_len = normalized_sequence.shape[0]
    query_full = jnp.dot(normalized_sequence, query_whole, preferred_element_type=jnp.float32)
    key_value_complete = jnp.einsum(
        "sd,dck->sck", normalized_sequence, keyval_whole, preferred_element_type=jnp.float32
    )
    context = attend(query_full, key_value_complete)
    return context.reshape(1, seq_len, context.shape[1])


def solution(mesh):
    in_specs = (
        P(None, "dp", None, "tensor"),
        P(),
        P(),
        P("dp", None, "tensor"),
        P("dp", None, "tensor"),
        P(),
        P("dp", "tensor"),
        P("dp", None, "tensor"),
        P(),
        P("dp"),
    )
    out_specs = P("dp", None, "tensor")
    return jax.shard_map(
        per_device, mesh=mesh, in_specs=in_specs, out_specs=out_specs, check_vma=False
    )
```

profile of v0, /device:TPU:13, one launch (start us, length us, event | category | flops | bytes accessed | tf_op | source)
XLA Modules:
  0.0 1217.2 jit_solution(16826153176477633601)
XLA Ops:
  6.5 2.0 copy.84
  8.6 0.8 copy-done.1
  9.4 3.9 copy.60
  13.3 0.6 copy-done.6
  14.1 0.1 reduce.2
  14.2 9.9 copy.58
  24.1 61.5 %all_gather.15 = bf16[8,8,2,3200]{1,0,2,3:T(8,128)(2,1)} all-gather(bf16[8,8,2,1600]{1,0,2,3:T(8,128)(2,1)} %copy.58), channel_id=1, replica_groups=mesh['dp'=16,'tensor'=2] {'tensor'}, dimensions={3}, use_global_device_ids=true | all-gather | bytes 1228800 | tf_op jit(solution)/shard_map/all_gather | solution.py:107
  85.6 11.9 copy.59
  97.5 1.4 convert_reduce_fusion
  99.0 1.5 fusion.22
  100.6 0.2 convert_reduce_fusion.1
  100.8 0.7 fusion.39
  101.5 0.2 select_reduce_fusion
  101.7 438.8 %all-gather.5.cloned.1.call-done = bf16[3200,2,4096]{2,0,1:T(8,128)(2,1)} async-done(((bf16[200,2,4096]{2,0,1:T(8,128)(2,1)}), bf16[3200,2,4096]{2,0,1:T(8,128)(2,1)}) %all-gather.5.cloned.1.call-update) | async-done | bytes 52428816 | tf_op jit(solution)/shard_map/all_gather | solution.py:85
  540.5 21.8 %fusion.12 = bf16[8,8,4096]{2,1,0:T(8,128)(2,1)} fusion(bf16[3200,2,4096]{2,0,1:T(8,128)(2,1)} %all-gather.5.cloned.1.call-done, bf16[8,8,2,3200]{3,1,0,2:T(8,128)(2,1)} %copy.59, f32[2,3200]{1,0:T(2,128)S(1)} %copy-done.3, f32[2,3200]{1,0:T(2,128)S(1)} %copy-done.4, f32[64]{0:T(128)S(1)} %rsqrt.20, f32[64]{0:T(128)S(1)} %div.47), kind=kOutput, calls=%fused_computation.20 | convolution fusion | flops 3358162944 | bytes 53824000 | tf_op jit(solution)/shard_map/rmf,fmo->ro/dot_general | solution.py:111
  562.3 1.1 broadcast.359
  563.4 2.7 scatter_fusion
  566.1 6.2 all-to-all-start
  573.0 0.7 iota_compare_fusion.2
  573.9 0.6 fusion.37
  574.5 22.7 %all-to-all-done = bf16[16,1,8,4096]{3,2,1,0:T(8,128)(2,1)} async-done(((bf16[16,1,8,4096]{3,2,1,0:T(8,128)(2,1)}), bf16[16,1,8,4096]{3,2,1,0:T(8,128)(2,1)}, u32[]{:S(2)}, u32[]{:S(2)}) %all-to-all-start) | async-done | bytes 1048608 | tf_op jit(solution)/shard_map/all_to_all | solution.py:116
  597.3 2.8 gather_fusion
  600.1 2.7 bitcast_select_fusion.4
  602.7 7.2 dynamic_update_slice.3
  610.0 1.7 copy-done
  611.7 2.4 copy.61
  614.2 0.5 all-gather.11.cloned.1.call-update
  614.7 0.7 iota_compare_fusion
  615.4 0.8 multiply_cosine_fusion
  616.2 13.1 %all-gather.7.cloned.1.call-done = bf16[384,8192]{1,0:T(8,128)(2,1)} async-done(((bf16[384,4096]{1,0:T(8,128)(2,1)}), bf16[384,8192]{1,0:T(8,128)(2,1)}) %all-gather.7.cloned.1.call-update) | async-done | bytes 6291472 | tf_op jit(solution)/shard_map/all_gather | solution.py:127
  629.3 4.1 fusion.1
  633.4 187.6 %all-gather.9.cloned.1.call-done = bf16[8192,2,512]{2,0,1:T(8,128)(2,1)} async-done(((bf16[512,2,512]{2,0,1:T(8,128)(2,1)}), bf16[8192,2,512]{2,0,1:T(8,128)(2,1)}) %all-gather.9.cloned.1.call-update) | async-done | bytes 16777232 | tf_op jit(solution)/shard_map/all_gather | solution.py:87
  821.0 12.1 fusion.5
  833.2 0.8 slice.40
  834.0 0.3 reshape_squeeze.4
  834.3 1.6 fusion.47
  835.9 336.2 %all-gather.11.cloned.1.call-done = bf16[8192,2048]{1,0:T(8,128)(2,1)} async-done(((bf16[512,2048]{1,0:T(8,128)(2,1)}), bf16[8192,2048]{1,0:T(8,128)(2,1)}) %all-gather.11.cloned.1.call-update) | async-done | bytes 33554448 | tf_op jit(solution)/shard_map/all_gather | solution.py:86
  1172.1 19.1 %convolution_bitcast_fusion.1 = f32[48,8,16,128]{3,1,2,0:T(8,128)S(1)} fusion(bf16[8192,2048]{1,0:T(8,128)(2,1)} %all-gather.11.cloned.1.call-done, bf16[384,8192]{1,0:T(8,128)(2,1)} %all-gather.7.cloned.1.call-done, f32[8192]{0:T(1024)} %param.15, f32[384]{0:T(512)S(1)} %add_rsqrt_fusion.1), kind=kOutput, calls=%fused_computation.26 | convolution fusion | flops 12897484800 | bytes 43025920 | tf_op jit(solution)/shard_map/dot_general | solution.py:134
  1191.2 0.7 copy.75
  1191.8 1.3 subtract_convert_fusion
  1193.1 0.4 copy.64
  1193.5 0.4 copy.65
  1193.9 1.9 copy.72
  1195.8 1.6 subtract_convert_fusion.1
  1197.4 1.5 fusion.23
  1199.0 5.4 fusion.48
  1204.3 4.7 fusion.15
  1209.1 1.6 copy.68
  (34 shorter events, 0.8 us)
Async XLA Ops:
  6.5 534.0 %all-gather.5.cloned.1.call-start = ((), (), s32[]{:S(2)}) async-start(), calls=%async_computation.1 | async-start | bytes 55705600 | tf_op jit(solution)/shard_map/all_gather | solution.py:85
  6.5 2.9 copy-start.1
  13.3 0.7 copy-start.6
  85.6 454.9 %copy-start.3 = (f32[2,3200]{1,0:T(2,128)S(1)}, f32[2,3200]{1,0:T(2,128)}, u32[]{:S(2)}) copy-start(f32[2,3200]{1,0:T(2,128)} %param.12) | copy-start | bytes 76804
  85.6 454.9 %copy-start.4 = (f32[2,3200]{1,0:T(2,128)S(1)}, f32[2,3200]{1,0:T(2,128)}, u32[]{:S(2)}) copy-start(f32[2,3200]{1,0:T(2,128)} %param.11) | copy-start | bytes 76804
  566.1 31.2 %all-to-all-start = ((bf16[16,1,8,4096]{3,2,1,0:T(8,128)(2,1)}), bf16[16,1,8,4096]{3,2,1,0:T(8,128)(2,1)}, u32[]{:S(2)}, u32[]{:S(2)}) async-start(bf16[16,1,8,4096]{3,2,1,0:T(8,128)(2,1)} %bitcast.86), calls=%async_computation | async-start | bytes 2097152 | tf_op jit(solution)/shard_map/all_to_all | solution.py:116
  572.3 56.9 %all-gather.7.cloned.1.call-start = ((), (), s32[]{:S(2)}) async-start(), calls=%async_computation.2 | async-start | bytes 9437184 | tf_op jit(solution)/shard_map/all_gather | solution.py:127
  610.0 1.7 copy-start
  611.7 209.3 %all-gather.9.cloned.1.call-start = ((), (), s32[]{:S(2)}) async-start(), calls=%async_computation.3 | async-start | bytes 17825792 | tf_op jit(solution)/shard_map/all_gather | solution.py:87
  614.1 558.0 %all-gather.11.cloned.1.call-start = ((), (), s32[]{:S(2)}) async-start(), calls=%async_computation.4 | async-start | bytes 35651584 | tf_op jit(solution)/shard_map/all_gather | solution.py:86
  615.4 205.6 %copy-start.7 = (f32[8192]{0:T(1024)S(1)}, f32[8192]{0:T(1024)}, u32[]{:S(2)}) copy-start(f32[8192]{0:T(1024)} %param.15) | copy-start | bytes 98308
  1197.4 1.5 copy-start.5
  1198.9 5.4 copy-start.2
Sparse Core Ops, SparseCore 0:
  13.4 527.0 all-gather.4
  611.8 17.4 all-gather.6
  632.0 188.9 all-gather.8
  823.6 348.4 all-gather.10
where the time goes:
time: 1230 us; the launch traced here: 1220 us
  waiting for transfers between devices  999 us (81%)
  blocking collectives  61.5 us (5%)
  matrix products  59.2 us (5%)
  local copies, waits for them, and re-layouts  55.2 us (4%)
  other arithmetic  21.9 us (2%)
  between operations  14 us (1%)
    all_gather x1, waiting for transfers between devices, per_device(): lax.all_gather(proj_weight, 'dp', axis=0, tiled=True)  439 us
    all_gather x1, waiting for transfers between devices, per_device(): lax.all_gather(w_query, 'dp', axis=0, tiled=True)  336 us
    all_gather x1, waiting for transfers between devices, per_device(): lax.all_gather(key_value_weight, 'dp', axis=0, tiled=True)  188 us
    all_gather x1, blocking collectives, per_device(): whole = lax.all_gather(vis_rows, 'tensor', axis=3, tiled=True)  61.5 us
  transfers between devices with their start and end apart: 5, of which 5 were waited for; matrix products, arithmetic and copies ran while one was open for 4% of the time, Pallas kernels for 0%

commit v1 on v0

--- a/solution.py
+++ b/solution.py
@@ -1,6 +1,11 @@
+import functools
+import math
+
 import jax
 import jax.numpy as jnp
 from jax import lax
+from jax.experimental import pallas as pl
+from jax.experimental.pallas import tpu as pltpu
 from jax.sharding import PartitionSpec as P
 
 QUERY_HEADS = 32
@@ -33,6 +38,146 @@
     centered = value_rows - average
     variance = jnp.mean(centered * centered, axis=(-2, -1), keepdims=True)
     return centered * lax.rsqrt(variance + vision_epsilon) * gain + bias_values
+
+
+MESH = pl.DeviceIdType.MESH
+
+
+def partner(data_index, step, inner, plane):
+    if plane is None:
+        return lax.rem(data_index + step, inner)
+    outer_at, inner_at = data_index // inner, data_index % inner
+    if plane:
+        return outer_at * inner + lax.rem(inner_at + step, inner)
+    count = lax.axis_size("dp") // inner
+    return lax.rem(outer_at + step, count) * inner + inner_at
+
+
+def place(data_index, inner, plane):
+    if plane is None:
+        return data_index
+    return data_index % inner if plane else data_index // inner
+
+
+def greet(size, inner, plane):
+    data_index = lax.axis_index("dp")
+    barrier = pltpu.get_barrier_semaphore()
+    for step in range(1, size):
+        pl.semaphore_signal(
+            barrier,
+            inc=1,
+            device_id={"dp": partner(data_index, step, inner, plane)},
+            device_id_type=MESH,
+        )
+    pl.semaphore_wait(barrier, size - 1)
+
+
+def exchange_kernel(size, inner, plane, x_ref, o_ref, send_sem, recv_sem, own_sem):
+    data_index = lax.axis_index("dp")
+    me = place(data_index, inner, plane)
+    own = pltpu.make_async_copy(x_ref.at[me], o_ref.at[me], own_sem)
+    own.start()
+    greet(size, inner, plane)
+    copies = []
+    for step in range(1, size):
+        target = partner(data_index, step, inner, plane)
+        copy = pltpu.make_async_remote_copy(
+            src_ref=x_ref.at[place(target, inner, plane)],
+            dst_ref=o_ref.at[me],
+            send_sem=send_sem.at[step - 1],
+            recv_sem=recv_sem.at[step - 1],
+            device_id={"dp": target},
+            device_id_type=MESH,
+        )
+        copy.start()
+        copies.append(copy)
+    own.wait()
+    for copy in copies:
+        copy.wait()
+
+
+def sum_kernel(size, inner, plane, rows, x_ref, o_ref, held, send_sem, recv_sem):
+    data_index = lax.axis_index("dp")
+    me = place(data_index, inner, plane)
+    greet(size, inner, plane)
+    copies = []
+    for step in range(1, size):
+        target = partner(data_index, step, inner, plane)
+        copy = pltpu.make_async_remote_copy(
+            src_ref=x_ref.at[place(target, inner, plane)],
+            dst_ref=held.at[step - 1],
+            send_sem=send_sem.at[step - 1],
+            recv_sem=recv_sem.at[step - 1],
+            device_id={"dp": target},
+            device_id_type=MESH,
+        )
+        copy.start()
+        copies.append(copy)
+    for copy in copies:
+        copy.wait_recv()
+
+    def add(at, carry):
+        window = pl.ds(pl.multiple_of(at * rows, rows), rows)
+        total = x_ref[me, window, :].astype(jnp.float32)
+        for step in range(1, size):
+            total = total + held[step - 1, window, :].astype(jnp.float32)
+        o_ref[window, :] = total.astype(o_ref.dtype)
+        return carry
+
+    lax.fori_loop(0, o_ref.shape[0] // rows, add, 0)
+    for copy in copies:
+        copy.wait_send()
+
+
+def exchange(blocks, inner, plane, number):
+    size = blocks.shape[0]
+    return pl.pallas_call(
+        functools.partial(exchange_kernel, size, inner, plane),
+        out_shape=jax.ShapeDtypeStruct(blocks.shape, blocks.dtype),
+        in_specs=[pl.BlockSpec(memory_space=pltpu.VMEM)],
+        out_specs=pl.BlockSpec(memory_space=pltpu.VMEM),
+        scratch_shapes=[
+            pltpu.SemaphoreType.DMA((size - 1,)),
+            pltpu.SemaphoreType.DMA((size - 1,)),
+            pltpu.SemaphoreType.DMA,
+        ],
+        compiler_params=pltpu.CompilerParams(
+            collective_id=number, has_side_effects=True, vmem_limit_bytes=40 << 20
+        ),
+        cost_estimate=pl.CostEstimate(
+            flops=0, bytes_accessed=40 * blocks.size, transcendentals=0
+        ),
+    )(blocks)
+
+
+def sum_blocks(blocks, inner, plane, number, kind):
+    size, rows, columns = blocks.shape
+    return pl.pallas_call(
+        functools.partial(sum_kernel, size, inner, plane, math.gcd(rows, 16)),
+        out_shape=jax.ShapeDtypeStruct((rows, columns), kind),
+        in_specs=[pl.BlockSpec(memory_space=pltpu.VMEM)],
+        out_specs=pl.BlockSpec(memory_space=pltpu.VMEM),
+        scratch_shapes=[
+            pltpu.VMEM((size - 1, rows, columns), blocks.dtype),
+            pltpu.SemaphoreType.DMA((size - 1,)),
+            pltpu.SemaphoreType.DMA((size - 1,)),
+        ],
+        compiler_params=pltpu.CompilerParams(
+            collective_id=number, has_side_effects=True, vmem_limit_bytes=40 << 20
+        ),
+        cost_estimate=pl.CostEstimate(
+            flops=0, bytes_accessed=40 * blocks.size, transcendentals=0
+        ),
+    )(blocks)
+
+
+def tensor_pieces(block):
+    count = lax.axis_size("tensor")
+    pieces = [block]
+    for step in range(1, count):
+        ring = [(at, (at + step) % count) for at in range(count)]
+        pieces.append(lax.ppermute(block, "tensor", ring))
+    return pieces
 
 
 def attend(query_full, key_value_complete):
@@ -77,15 +222,19 @@
 ):
     data_count = lax.axis_size("dp")
     data_index = lax.axis_index("dp")
+    tensor_count = lax.axis_size("tensor")
+    tensor_index = lax.axis_index("tensor")
     tile_rows, tile_tok, merge_count, part_width = vis_rows.shape
     vision_width = ln_gain.shape[1]
     part_model = proj_weight.shape[2]
     token_count = tile_rows * tile_tok
-    proj_whole, query_whole, keyval_whole = (
-        lax.all_gather(proj_weight, "dp", axis=0, tiled=True),
-        lax.all_gather(w_query, "dp", axis=0, tiled=True),
-        lax.all_gather(key_value_weight, "dp", axis=0, tiled=True),
-    )
+    inner = 1 << (int(math.log2(data_count)) // 2)
+    outer = data_count // inner
+    columns_of = [[at * inner + b for at in range(outer)] for b in range(inner)]
+    depth = w_query.shape[0]
+    weight = jnp.concatenate([w_query, key_value_weight.reshape(depth, -1)], axis=1)
+    weight = lax.all_gather(weight, "dp", axis=0, tiled=True, axis_index_groups=columns_of)
+
     max_tiles = 2 * tile_rows
     slot_count = (max_tiles + data_count - 1) // data_count
     tile_ends = jnp.cumsum(tile_counts)
@@ -104,18 +253,34 @@
     sources = (my_first + tile_order) % data_count
     slot_index = tile_order // data_count
     image_span = max_tiles * tile_tok
-    whole = lax.all_gather(vis_rows, "tensor", axis=3, tiled=True)
-    merged = whole.reshape(token_count, merge_count, vision_width).astype(jnp.float32)
-    normed_vis = layer_norm(merged, ln_gain, ln_bias).astype(jnp.bfloat16)
-    image_cols = (
-        jnp.einsum("rmf,fmo->ro", normed_vis, proj_whole, preferred_element_type=jnp.float32)
-        .astype(jnp.bfloat16)
-        .reshape(tile_rows, tile_tok, part_model)
-    )
+
+    pieces = tensor_pieces(vis_rows.reshape(token_count, merge_count, part_width))
+    whole = jnp.zeros((token_count, merge_count, vision_width), vis_rows.dtype)
+    for step, piece in enumerate(pieces):
+        start = (tensor_index - step) % tensor_count * part_width
+        whole = lax.dynamic_update_slice_in_dim(whole, piece, start, 2)
+    normed_vis = layer_norm(whole.astype(jnp.float32), ln_gain, ln_bias).astype(jnp.bfloat16)
+    feature = vision_width // data_count
+    blocks = normed_vis.reshape(token_count, merge_count, data_count, feature)
+    blocks = blocks.transpose(2, 0, 1, 3).reshape(data_count, token_count, merge_count * feature)
+    blocks = exchange(blocks, data_count, None, 0)
+    proj = proj_weight.transpose(1, 0, 2).reshape(merge_count * feature, part_model)
+    partial = jnp.dot(
+        blocks.reshape(data_count * token_count, merge_count * feature),
+        proj,
+        preferred_element_type=jnp.float32,
+    ).astype(jnp.bfloat16)
+    partial = partial.reshape(outer, inner, token_count, part_model).transpose(1, 0, 2, 3)
+    partial = sum_blocks(
+        partial.reshape(inner, outer * token_count, part_model), inner, True, 1, jnp.bfloat16
+    )
+    image_cols = sum_blocks(
+        partial.reshape(outer, token_count, part_model), inner, False, 2, jnp.bfloat16
+    ).reshape(tile_rows, tile_tok, part_model)
+
     empty_slots = jnp.zeros((data_count, slot_count) + image_cols.shape[1:], jnp.bfloat16)
-    received = lax.all_to_all(
-        empty_slots.at[owners, slots].set(image_cols), "dp", split_axis=0, concat_axis=0, tiled=True
-    )
+    routed = empty_slots.at[owners, slots].set(image_cols)
+    received = exchange(routed, data_count, None, 3)
     arrived = received[sources, slot_index]
     arrived = arrived.reshape(image_span, part_model)
     start_row = image_offsets[0]
@@ -124,18 +289,29 @@
     is_image = jnp.repeat(tile_order < my_count, tile_tok)[:, None]
     combined = jnp.where(is_image, arrived, current)
     sequence = lax.dynamic_update_slice_in_dim(sequence, combined, start_row, 0)
-    gathered = lax.all_gather(sequence, "tensor", axis=1, tiled=True)
-    seq_float = gathered.astype(jnp.float32)
-    mean_square = jnp.mean(seq_float * seq_float, axis=-1, keepdims=True)
-    normalized_sequence = (seq_float * lax.rsqrt(mean_square + decoder_epsilon) * attn_gain).astype(
-        jnp.bfloat16
-    )
-    seq_len = normalized_sequence.shape[0]
-    query_full = jnp.dot(normalized_sequence, query_whole, preferred_element_type=jnp.float32)
-    key_value_complete = jnp.einsum(
-        "sd,dck->sck", normalized_sequence, keyval_whole, preferred_element_type=jnp.float32
-    )
-    context = attend(query_full, key_value_complete)
+
+    seq_len = sequence.shape[0]
+    model_width = attn_gain.shape[0]
+    seq_float = sequence.astype(jnp.float32)
+    squares = lax.psum(jnp.sum(seq_float * seq_float, axis=-1), "tensor")[:, None]
+    gain = lax.dynamic_slice_in_dim(attn_gain, tensor_index * part_model, part_model, 0)
+    normalized = (
+        seq_float * lax.rsqrt(squares / model_width + decoder_epsilon) * gain
+    ).astype(jnp.bfloat16)
+    held_rows = part_model // depth // inner
+    normalized = normalized.reshape(seq_len, held_rows, inner, depth).transpose(2, 0, 1, 3)
+    normalized = exchange(
+        normalized.reshape(inner, seq_len, held_rows * depth), inner, True, 4
+    ).reshape(inner * seq_len, held_rows * depth)
+    product = 0.0
+    for step, piece in enumerate(tensor_pieces(normalized)):
+        start = (tensor_index - step) % tensor_count * (held_rows * depth)
+        rows = lax.dynamic_slice_in_dim(weight, start, held_rows * depth, 0)
+        product = product + jnp.dot(piece, rows, preferred_element_type=jnp.float32)
+    product = product.astype(jnp.bfloat16).reshape(inner, seq_len, -1)
+    product = sum_blocks(product, inner, True, 5, jnp.float32)
+    part_query = w_query.shape[1]
+    context = attend(product[:, :part_query], product[:, part_query:].reshape(seq_len, 2, -1))
     return context.reshape(1, seq_len, context.shape[1])
 
 

time: 1230 us -> 596 us (0.48)
  waiting for transfers between devices: 999 us -> 0.04 us
  Pallas kernels: 0 us -> 408 us
  blocking collectives: 61.5 us -> 4.17 us
  local copies, waits for them, and re-layouts: 55.2 us -> 93.5 us
    all_gather x4 -> x1, waiting for transfers between devices: 976 us -> 0.02 us  [per_device(): lax.all_gather(weight, 'dp', axis=0, tiled=True, axis_index_groups=column...]
    pallas_call x0 -> x6, Pallas kernels: none -> 408 us  [the longest x3 290 us: sum_blocks(): pl.pallas_call(functools.partial(sum_kernel, size, inner, plane, math.gcd...]
    all_gather x1 -> x0, blocking collectives: 61.5 us -> none  [per_device(): whole = lax.all_gather(vis_rows, 'tensor', axis=3, tiled=True)]
    reshape x0 -> x8, local copies, waits for them, and re-layouts: none -> 30.9 us  [the longest x2 9.08 us: per_device(): normalized.reshape(seq_len, held_rows, inner, depth).transpose(2, 0, 1, 3)]
    all_to_all x1 -> x0, waiting for transfers between devices: 22.7 us -> none  [per_device(): lax.all_to_all(empty_slots.at[owners, slots].set(image_cols), 'dp', split...]
    dynamic_update_slice x0 -> x2, local copies, waits for them, and re-layouts: none -> 13.1 us  [per_device(): whole = lax.dynamic_update_slice_in_dim(whole, piece, start, 2)]
  transfers between devices with their start and end apart: 5 -> 3, of which waited for: 5 -> 0; matrix products, arithmetic and copies ran while one was open for 4% -> 16% of each run, Pallas kernels for 0% -> 51%
where the time goes in v1:
time: 596 us; the launch traced here: 592 us
  Pallas kernels  408 us (68%)
  local copies, waits for them, and re-layouts  93.5 us (16%)
  matrix products  48.6 us (8%)
  other arithmetic  21.4 us (4%)
  between operations  14.8 us (2%)
    pallas_call x3, Pallas kernels, sum_blocks(): pl.pallas_call(functools.partial(sum_kernel, size, inner, plane, math.gcd...  290 us
    pallas_call x3, Pallas kernels, exchange(): pl.pallas_call(functools.partial(exchange_kernel, size, inner, plane), ou...  118 us
    dot_general x2, matrix products, per_device(): product = product + jnp.dot(piece, rows, preferred_element_type=jnp.float32)  33.7 us
    unnamed x30, local copies, waits for them, and re-layouts  23.7 us
    dynamic_update_slice x2, local copies, waits for them, and re-layouts, per_device(): whole = lax.dynamic_update_slice_in_dim(whole, piece, start, 2)  13.1 us
  transfers between devices with their start and end apart: 3, of which 0 were waited for; matrix products, arithmetic and copies ran while one was open for 16% of the time, Pallas kernels for 51%

profile of v1, /device:TPU:13, one launch (start us, length us, event | category | flops | bytes accessed | tf_op | source)
XLA Modules:
  0.0 591.8 jit_solution(10013944406729139285)
XLA Ops:
  6.5 4.1 copy.65
  10.9 1.9 pad_maximum_fusion
  12.9 2.0 copy.35
  14.8 0.7 collective-permute-start
  15.5 4.0 copy.38
  22.0 6.9 %dynamic_update_slice.9 = bf16[64,2,3200]{2,0,1:T(8,128)(2,1)S(1)} dynamic-update-slice(bf16[64,2,3200]{2,0,1:T(8,128)(2,1)S(1)} %broadcast_in_dim.48, bf16[64,2,1600]{2,0,1:T(8,128)(2,1)} %copy.35, s32[]{:T(128)} %constant.94.clone.1, s32[]{:T(128)} %constant.94.clone.1, s32[]{:T(128)S(6)} %select_n.136) | dynamic-update-slice | bytes 819204 | tf_op jit(solution)/shard_map/dynamic_update_slice | solution.py:261
  30.0 6.1 %dynamic_update_slice.10 = bf16[64,2,3200]{2,0,1:T(8,128)(2,1)S(1)} dynamic-update-slice(bf16[64,2,3200]{2,0,1:T(8,128)(2,1)S(1)} %dynamic_update_slice.9, bf16[64,2,1600]{2,0,1:T(8,128)(2,1)} %collective-permute-done, s32[]{:T(128)} %constant.94.clone.1, s32[]{:T(128)} %constant.94.clone.1, s32[]{:T(128)S(6)} %select_n.138) | dynamic-update-slice | bytes 819204 | tf_op jit(solution)/shard_map/dynamic_update_slice | solution.py:261
  37.2 3.1 reshape.355
  40.3 1.1 copy.37
  42.1 52.6 %shard_map.100 = bf16[16,64,400]{2,1,0:T(8,128)(2,1)S(1)} custom-call(bf16[16,64,400]{2,1,0:T(8,128)(2,1)S(1)} %reshape.356.x_ref), custom_call_target="tpu_custom_call" | custom-call | bytes 16384000 | tf_op jit(solution)/shard_map/pallas_call | solution.py:134
  94.7 8.7 %convolution_convert_fusion = bf16[1024,4096]{1,0:T(8,128)(2,1)} fusion(bf16[1024,400]{1,0:T(8,128)(2,1)S(1)} %bitcast.86, bf16[400,4096]{1,0:T(8,128)(2,1)} %bitcast.95), kind=kOutput, calls=%fused_computation.9 | convolution fusion | flops 3359637504 | bytes 12484608 | tf_op jit(solution)/shard_map/dot_general | solution.py:268
  103.3 7.7 %copy.39 = bf16[4,4,64,4096]{3,2,0,1:T(8,128)(2,1)} copy(bf16[4,4,64,4096]{3,2,1,0:T(8,128)(2,1)} %bitcast.90) | data formatting | bytes 16777216 | tf_op jit(solution)/shard_map/reshape | solution.py:273
  111.1 3.5 copy-done
  114.5 104.9 %shard_map.101 = bf16[256,4096]{1,0:T(8,128)(2,1)S(1)} custom-call(bf16[4,256,4096]{2,1,0:T(8,128)(2,1)S(1)} %bitcast.81), custom_call_target="tpu_custom_call" | custom-call | bytes 167772160 | tf_op jit(solution)/shard_map/pallas_call | solution.py:155
  219.4 79.5 %shard_map.102 = bf16[64,4096]{1,0:T(8,128)(2,1)S(1)} custom-call(bf16[4,64,4096]{2,1,0:T(8,128)(2,1)S(1)} %bitcast.83), custom_call_target="tpu_custom_call" | custom-call | bytes 41943040 | tf_op jit(solution)/shard_map/pallas_call | solution.py:155
  299.1 0.8 scatter_fusion
  299.9 25.2 %shard_map.103 = bf16[16,1,8,4096]{3,2,1,0:T(8,128)(2,1)S(1)} custom-call(bf16[16,1,8,4096]{3,2,1,0:T(8,128)(2,1)S(1)} %bitcast.84), custom_call_target="tpu_custom_call" | custom-call | bytes 20971520 | tf_op jit(solution)/shard_map/pallas_call | solution.py:134
  325.1 1.6 gather_fusion
  326.7 3.2 bitcast_select_fusion.4
  329.8 7.3 %dynamic_update_slice.11 = bf16[384,4096]{1,0:T(8,128)(2,1)S(1)} dynamic-update-slice(bf16[384,4096]{1,0:T(8,128)(2,1)S(1)} %bitcast.87, bf16[128,4096]{1,0:T(8,128)(2,1)} %bitcast_select_fusion.4, s32[]{:T(128)S(6)} %select_n.144, s32[]{:T(128)} %constant.94.clone.1) | dynamic-update-slice | bytes 2097156 | tf_op jit(solution)/shard_map/dynamic_update_slice | solution.py:291
  337.1 0.7 fusion.2
  337.8 4.2 psum.7
  342.0 2.7 fusion.4
  344.7 5.0 reshape.364
  349.6 4.1 copy.58
  353.7 4.7 reshape.365.x_ref
  358.4 39.8 %shard_map.104 = bf16[4,384,1024]{2,1,0:T(8,128)(2,1)} custom-call(bf16[4,384,1024]{2,1,0:T(8,128)(2,1)S(1)} %reshape.365.x_ref), custom_call_target="tpu_custom_call" | custom-call | bytes 62914560 | tf_op jit(solution)/shard_map/pallas_call | solution.py:134
  398.8 0.7 iota_compare_fusion
  399.5 0.8 multiply_cosine_fusion
  400.3 16.7 %fusion.6 = f32[1536,3072]{1,0:T(8,128)} fusion(bf16[1536,1024]{1,0:T(8,128)(2,1)} %bitcast.21, bf16[2048,3072]{1,0:T(8,128)(2,1)} %all-gather.2.cloned.1.call-done, s32[]{:T(128)S(6)} %select_n.147), kind=kOutput, calls=%fused_computation.15 | convolution fusion | flops 9663676416 | bytes 28311556 | tf_op jit(solution)/shard_map/dot_general | solution.py:310
  417.0 17.0 %add_convert_fusion = bf16[1536,3072]{1,0:T(8,128)(2,1)} fusion(f32[1536,3072]{1,0:T(8,128)} %fusion.6, bf16[1536,1024]{1,0:T(8,128)(2,1)S(1)} %collective-permute-done.1, bf16[2048,3072]{1,0:T(8,128)(2,1)} %all-gather.2.cloned.1.call-done, s32[]{:T(128)S(6)} %select_n.148), kind=kOutput, calls=%fused_computation.3 | convolution fusion | flops 9673113600 | bytes 37748740 | tf_op jit(solution)/shard_map/dot_general | solution.py:310
  434.0 3.7 copy-done.1
  437.7 106.0 %shard_map.105 = f32[384,3072]{1,0:T(8,128)S(1)} custom-call(bf16[4,384,3072]{2,1,0:T(8,128)(2,1)S(1)} %bitcast.82), custom_call_target="tpu_custom_call" | custom-call | bytes 188743680 | tf_op jit(solution)/shard_map/pallas_call | solution.py:155
  543.7 1.3 slice.25
  545.2 3.7 reshape.369
  548.9 2.8 slice.38
  551.7 3.1 slice.49
  554.8 3.0 copy.52
  557.8 2.0 fusion.40
  559.9 2.1 copy.53
  562.0 2.2 copy.54
  564.9 1.3 subtract_convert_fusion
  566.9 2.9 copy.41
  569.9 1.6 subtract_convert_fusion.1
  571.4 1.5 fusion.19
  573.0 5.1 fusion.41
  578.1 4.7 fusion.14
  582.8 1.6 copy.48
  (56 shorter events, 7.1 us)
Async XLA Ops:
  6.5 4.4 copy-start.4
  6.5 4.1 copy-start.5
  6.5 393.7 %all-gather.2.cloned.1.call-start = ((), (), s32[]{:S(2)}) async-start(), calls=%async_computation | async-start | bytes 15728640 | tf_op jit(solution)/shard_map/all_gather | solution.py:236
  12.8 2.7 copy-start.3
  14.8 15.2 %collective-permute-start = (bf16[64,2,1600]{2,0,1:T(8,128)(2,1)}, bf16[64,2,1600]{2,0,1:T(8,128)(2,1)}, u32[]{:S(2)}, u32[]{:S(2)}) collective-permute-start(bf16[64,2,1600]{2,0,1:T(8,128)(2,1)} %copy.35), channel_id=1, source_target_pairs={{0,1},{1,0},{2,3},{3,2},{4,5},{5,4},{6,7},{7,6},{8,9},{9,8},{10,11... | collective-permute-start | bytes 1228808 | tf_op jit(solution)/shard_map/ppermute | solution.py:179
  15.5 4.0 copy-start.10
  19.5 17.3 %copy-start.8 = (f32[2,3200]{1,0:T(2,128)S(1)}, f32[2,3200]{1,0:T(2,128)}, u32[]{:S(2)}) copy-start(f32[2,3200]{1,0:T(2,128)} %param.12) | copy-start | bytes 76804
  19.5 17.3 %copy-start.9 = (f32[2,3200]{1,0:T(2,128)S(1)}, f32[2,3200]{1,0:T(2,128)}, u32[]{:S(2)}) copy-start(f32[2,3200]{1,0:T(2,128)} %param.11) | copy-start | bytes 76804
  111.1 3.5 copy-start
  326.7 3.2 copy-start.2
  329.8 12.1 %dynamic-slice-start = ((f32[8192]{0:T(1024)}, s32[]{:T(128)}), f32[4096]{0:T(1024)S(1)}, s32[]{:S(2)}) async-start(f32[8192]{0:T(1024)} %param.15, s32[]{:T(128)} %select_n.146), calls=%async_computation.1 | async-start | bytes 33280 | tf_op jit(solution)/shard_map/dynamic_slice | solution.py:297
  398.2 18.8 %collective-permute-start.1 = (bf16[1536,1024]{1,0:T(8,128)(2,1)}, bf16[1536,1024]{1,0:T(8,128)(2,1)S(1)}, u32[]{:S(2)}, u32[]{:S(2)}) collective-permute-start(bf16[1536,1024]{1,0:T(8,128)(2,1)} %bitcast.21), channel_id=1, source_target_pairs={{0,1},{1,0},{2,3},{3,2},{4,5},{5,4},{6,7},{7,6},{8,9},{9,8},{10,11... | collective-permute-start | bytes 9437192 | tf_op jit(solution)/shard_map/ppermute | solution.py:179
  434.0 3.7 copy-start.1
  571.4 1.5 copy-start.7
  573.0 5.2 copy-start.6
Sparse Core Ops, SparseCore 0:
  13.0 282.1 all-gather.1

commit v2 on v1

--- a/solution.py
+++ b/solution.py
@@ -16,21 +16,6 @@
 vision_epsilon = 1e-06
 decoder_epsilon = 1e-05
 rope_base = 500000.0
-
-
-def apply_rotary(value_rows, position_indices):
-    half_width = value_rows.shape[-1] // 2
-    exponents = jnp.arange(half_width, dtype=jnp.float32) * (2.0 / value_rows.shape[-1])
-    frequency = rope_base ** (-exponents)
-    angles = position_indices.astype(jnp.float32)[:, None] * frequency[None, :]
-    cosine = jnp.cos(angles)[:, None, :]
-    sine = jnp.sin(angles)[:, None, :]
-    first_half = value_rows[..., :half_width]
-    second_half = value_rows[..., half_width:]
-    return jnp.concatenate(
-        [first_half * cosine - second_half * sine, second_half * cosine + first_half * sine],
-        axis=-1,
-    )
 
 
 def layer_norm(value_rows, gain, bias_values):
@@ -96,37 +81,200 @@
         copy.wait()
 
 
-def sum_kernel(size, inner, plane, rows, x_ref, o_ref, held, send_sem, recv_sem):
-    data_index = lax.axis_index("dp")
-    me = place(data_index, inner, plane)
-    greet(size, inner, plane)
+def greet_both(inner):
+    data_index = lax.axis_index("dp")
+    outer = lax.axis_size("dp") // inner
+    barrier = pltpu.get_barrier_semaphore()
+    for plane, size in ((True, inner), (False, outer)):
+        for step in range(1, size):
+            pl.semaphore_signal(
+                barrier,
+                inc=1,
+                device_id={"dp": partner(data_index, step, inner, plane)},
+                device_id_type=MESH,
+            )
+    pl.semaphore_wait(barrier, inner + outer - 2)
+
+
+def reduce_kernel(
+    inner, chunks, rows, x_ref, o_ref, held, mid, got, send_1, recv_1, send_2, recv_2
+):
+    data_index = lax.axis_index("dp")
+    outer, tokens, columns = mid.shape
+    wide = columns // chunks
+    me, me_outer = place(data_index, inner, True), place(data_index, inner, False)
+    greet_both(inner)
+    first, second = {}, {}
+    for chunk in range(chunks):
+        part = pl.ds(chunk * wide, wide)
+        for step in range(1, inner):
+            target = partner(data_index, step, inner, True)
+            first[chunk, step] = pltpu.make_async_remote_copy(
+                src_ref=x_ref.at[:, place(target, inner, True), :, part],
+                dst_ref=held.at[step - 1, :, :, part],
+                send_sem=send_1.at[step - 1, chunk],
+                recv_sem=recv_1.at[step - 1, chunk],
+                device_id={"dp": target},
+                device_id_type=MESH,
+            )
+            first[chunk, step].start()
+    for chunk in range(chunks):
+        part = pl.ds(chunk * wide, wide)
+        for step in range(1, inner):
+            first[chunk, step].wait_recv()
+
+        def add(at, carry):
+            row = lax.rem(me_outer + 1 + at // (tokens // rows), outer)
+            window = pl.ds(pl.multiple_of(at % (tokens // rows) * rows, rows), rows)
+            total = x_ref[row, me, window, part].astype(jnp.float32)
+            for step in range(1, inner):
+                total = total + held[step - 1, row, window, part].astype(jnp.float32)
+            mid[row, window, part] = total.astype(mid.dtype)
+            return carry
+
+        lax.fori_loop(0, outer * (tokens // rows), add, 0)
+        for step in range(1, outer):
+            target = partner(data_index, step, inner, False)
+            second[chunk, step] = pltpu.make_async_remote_copy(
+                src_ref=mid.at[place(target, inner, False), :, part],
+                dst_ref=got.at[step - 1, :, part],
+                send_sem=send_2.at[step - 1, chunk],
+                recv_sem=recv_2.at[step - 1, chunk],
+                device_id={"dp": target},
+                device_id_type=MESH,
+            )
+            second[chunk, step].start()
+    for chunk in range(chunks):
+        part = pl.ds(chunk * wide, wide)
+        for step in range(1, outer):
+            second[chunk, step].wait_recv()
+
+        def finish(at, carry):
+            window = pl.ds(pl.multiple_of(at * rows, rows), rows)
+            total = mid[me_outer, window, part].astype(jnp.float32)
+            for step in range(1, outer):
+                total = total + got[step - 1, window, part].astype(jnp.float32)
+            o_ref[window, part] = total.astype(o_ref.dtype)
+            return carry
+
+        lax.fori_loop(0, tokens // rows, finish, 0)
+    for copy in list(first.values()) + list(second.values()):
+        copy.wait_send()
+
+
+def reduce_blocks(partial, number):
+    outer, inner, tokens, columns = partial.shape
+    chunks = 4
+    return pl.pallas_call(
+        functools.partial(reduce_kernel, inner, chunks, math.gcd(tokens, 16)),
+        out_shape=jax.ShapeDtypeStruct((tokens, columns), partial.dtype),
+        in_specs=[pl.BlockSpec(memory_space=pltpu.VMEM)],
+        out_specs=pl.BlockSpec(memory_space=pltpu.VMEM),
+        scratch_shapes=[
+            pltpu.VMEM((inner - 1, outer, tokens, columns), partial.dtype),
+            pltpu.VMEM((outer, tokens, columns), partial.dtype),
+            pltpu.VMEM((outer - 1, tokens, columns), partial.dtype),
+            pltpu.SemaphoreType.DMA((inner - 1, chunks)),
+            pltpu.SemaphoreType.DMA((inner - 1, chunks)),
+            pltpu.SemaphoreType.DMA((outer - 1, chunks)),
+            pltpu.SemaphoreType.DMA((outer - 1, chunks)),
+        ],
+        compiler_params=pltpu.CompilerParams(
+            collective_id=number, has_side_effects=True, vmem_limit_bytes=40 << 20
+        ),
+        cost_estimate=pl.CostEstimate(
+            flops=0, bytes_accessed=60 * partial.size, transcendentals=0
+        ),
+    )(partial)
+
+
+def product_kernel(inner, count, tile, rows, *refs):
+    a_refs = refs[:count]
+    w_ref, o_ref, leaving, held, send_sem, recv_sem = refs[count:]
+    depth = w_ref.shape[0] // count
+    tensor_index = lax.axis_index("tensor")
+    data_index = lax.axis_index("dp")
+    tiles = o_ref.shape[1] // tile
+
+    def compute(block, dst_ref, low, high):
+        def one(at, carry):
+            part = pl.ds(pl.multiple_of(at * tile, tile), tile)
+            total = None
+            for ahead, a_ref in enumerate(a_refs):
+                start = lax.rem(tensor_index + count - ahead, count) * depth
+                rows_at = pl.ds(pl.multiple_of(start, depth), depth)
+                term = jnp.dot(
+                    a_ref[block], w_ref[rows_at, part], preferred_element_type=jnp.float32
+                )
+                total = term if total is None else total + term
+            dst_ref[:, part] = total.astype(dst_ref.dtype)
+            return carry
+
+        lax.fori_loop(low, high, one, 0)
+
+    greet(inner, inner, True)
     copies = []
-    for step in range(1, size):
-        target = partner(data_index, step, inner, plane)
-        copy = pltpu.make_async_remote_copy(
-            src_ref=x_ref.at[place(target, inner, plane)],
-            dst_ref=held.at[step - 1],
-            send_sem=send_sem.at[step - 1],
-            recv_sem=recv_sem.at[step - 1],
-            device_id={"dp": target},
-            device_id_type=MESH,
-        )
-        copy.start()
-        copies.append(copy)
+    for step in range(1, inner + 1):
+        target = partner(data_index, step, inner, True)
+        block = place(target, inner, True)
+        dst_ref = leaving.at[step - 1] if step < inner else o_ref
+        compute(block, dst_ref, 0, 1)
+        if copies:
+            copies[-1].start()
+        compute(block, dst_ref, 1, tiles)
+        if step < inner:
+            copies.append(
+                pltpu.make_async_remote_copy(
+                    src_ref=leaving.at[step - 1],
+                    dst_ref=held.at[step - 1],
+                    send_sem=send_sem.at[step - 1],
+                    recv_sem=recv_sem.at[step - 1],
+                    device_id={"dp": target},
+                    device_id_type=MESH,
+                )
+            )
     for copy in copies:
         copy.wait_recv()
 
     def add(at, carry):
         window = pl.ds(pl.multiple_of(at * rows, rows), rows)
-        total = x_ref[me, window, :].astype(jnp.float32)
-        for step in range(1, size):
+        total = o_ref[window, :]
+        for step in range(1, inner):
             total = total + held[step - 1, window, :].astype(jnp.float32)
-        o_ref[window, :] = total.astype(o_ref.dtype)
+        o_ref[window, :] = total
         return carry
 
     lax.fori_loop(0, o_ref.shape[0] // rows, add, 0)
     for copy in copies:
         copy.wait_send()
+
+
+def product_blocks(pieces, weight, number):
+    inner, rows, depth = pieces[0].shape
+    columns = weight.shape[1]
+    count = len(pieces)
+    return pl.pallas_call(
+        functools.partial(
+            product_kernel, inner, count, math.gcd(columns, 512), math.gcd(rows, 16)
+        ),
+        out_shape=jax.ShapeDtypeStruct((rows, columns), jnp.float32),
+        in_specs=[pl.BlockSpec(memory_space=pltpu.VMEM)] * (count + 1),
+        out_specs=pl.BlockSpec(memory_space=pltpu.VMEM),
+        scratch_shapes=[
+            pltpu.VMEM((inner - 1, rows, columns), jnp.bfloat16),
+            pltpu.VMEM((inner - 1, rows, columns), jnp.bfloat16),
+            pltpu.SemaphoreType.DMA((inner - 1,)),
+            pltpu.SemaphoreType.DMA((inner - 1,)),
+        ],
+        compiler_params=pltpu.CompilerParams(
+            collective_id=number, has_side_effects=True, vmem_limit_bytes=56 << 20
+        ),
+        cost_estimate=pl.CostEstimate(
+            flops=2 * count * inner * rows * depth * columns,
+            bytes_accessed=200 << 20,
+            transcendentals=0,
+        ),
+    )(*pieces, weight)
 
 
 def exchange(blocks, inner, plane, number):
@@ -150,27 +298,6 @@
     )(blocks)
 
 
-def sum_blocks(blocks, inner, plane, number, kind):
-    size, rows, columns = blocks.shape
-    return pl.pallas_call(
-        functools.partial(sum_kernel, size, inner, plane, math.gcd(rows, 16)),
-        out_shape=jax.ShapeDtypeStruct((rows, columns), kind),
-        in_specs=[pl.BlockSpec(memory_space=pltpu.VMEM)],
-        out_specs=pl.BlockSpec(memory_space=pltpu.VMEM),
-        scratch_shapes=[
-            pltpu.VMEM((size - 1, rows, columns), blocks.dtype),
-            pltpu.SemaphoreType.DMA((size - 1,)),
-            pltpu.SemaphoreType.DMA((size - 1,)),
-        ],
-        compiler_params=pltpu.CompilerParams(
-            collective_id=number, has_side_effects=True, vmem_limit_bytes=40 << 20
-        ),
-        cost_estimate=pl.CostEstimate(
-            flops=0, bytes_accessed=40 * blocks.size, transcendentals=0
-        ),
-    )(blocks)
-
-
 def tensor_pieces(block):
     count = lax.axis_size("tensor")
     pieces = [block]
@@ -180,32 +307,59 @@
     return pieces
 
 
-def attend(query_full, key_value_complete):
-    seq_len = query_full.shape[0]
-    query_group_count = QUERY_HEADS // KEY_VALUE_HEADS
-    local_kv = key_value_complete.shape[2] // HEAD_WIDTH
-    local_query = query_full.shape[1] // HEAD_WIDTH
-    position_indices = jnp.arange(seq_len, dtype=jnp.int32)
-    query_rows = apply_rotary(
-        query_full.reshape(seq_len, local_query, HEAD_WIDTH), position_indices
-    ).astype(jnp.bfloat16)
-    query_rows = query_rows.reshape(seq_len, local_kv, query_group_count, HEAD_WIDTH)
-    key_rows = apply_rotary(
-        key_value_complete[:, 0].reshape(seq_len, local_kv, HEAD_WIDTH), position_indices
-    ).astype(jnp.bfloat16)
-    value_rows = (
-        key_value_complete[:, 1].reshape(seq_len, local_kv, HEAD_WIDTH).astype(jnp.bfloat16)
-    )
-    scores = jnp.einsum(
-        "pgjd,kgd->gjpk", query_rows, key_rows, preferred_element_type=jnp.float32
-    ) * HEAD_WIDTH ** (-0.5)
-    causal = position_indices[:, None] >= position_indices[None, :]
-    scores = jnp.where(causal[None, None], scores, -1e30)
-    row_max = jnp.max(scores, axis=-1, keepdims=True)
-    exponentials = jnp.exp(scores - row_max)
-    weights = (exponentials / jnp.sum(exponentials, axis=-1, keepdims=True)).astype(jnp.bfloat16)
-    context = jnp.einsum("gjpk,kgd->pgjd", weights, value_rows, preferred_element_type=jnp.float32)
-    return context.astype(jnp.bfloat16).reshape(seq_len, local_query * HEAD_WIDTH)
+def attend_kernel(group, q_ref, k_ref, v_ref, cos_ref, sin_ref, o_ref):
+    cosine, sine = cos_ref[...], sin_ref[...]
+
+    def turn(rows):
+        return (rows * cosine + pltpu.roll(rows, HEAD_WIDTH // 2, 1) * sine).astype(jnp.bfloat16)
+
+    key_rows = turn(k_ref[...])
+    value_rows = v_ref[...].astype(jnp.bfloat16)
+    seq_len = key_rows.shape[0]
+    row_at = lax.broadcasted_iota(jnp.int32, (seq_len, seq_len), 0)
+    column_at = lax.broadcasted_iota(jnp.int32, (seq_len, seq_len), 1)
+    for head in range(group):
+        part = pl.ds(head * HEAD_WIDTH, HEAD_WIDTH)
+        query_rows = turn(q_ref[:, part])
+        scores = lax.dot_general(
+            query_rows, key_rows, (((1,), (1,)), ((), ())), preferred_element_type=jnp.float32
+        ) * HEAD_WIDTH ** (-0.5)
+        scores = jnp.where(row_at >= column_at, scores, -1e30)
+        exponentials = jnp.exp(scores - jnp.max(scores, axis=-1, keepdims=True))
+        weights = exponentials / jnp.sum(exponentials, axis=-1, keepdims=True)
+        context = jnp.dot(
+            weights.astype(jnp.bfloat16), value_rows, preferred_element_type=jnp.float32
+        )
+        o_ref[:, part] = context.astype(o_ref.dtype)
+
+
+def attend(product, part_query):
+    seq_len, columns = product.shape
+    group = QUERY_HEADS // KEY_VALUE_HEADS
+    local_kv = part_query // HEAD_WIDTH // group
+    key_at = part_query // HEAD_WIDTH
+    half_width = HEAD_WIDTH // 2
+    exponents = jnp.arange(half_width, dtype=jnp.float32) * (2.0 / HEAD_WIDTH)
+    frequency = rope_base ** (-exponents)
+    angles = jnp.arange(seq_len, dtype=jnp.float32)[:, None] * frequency[None, :]
+    cosine, sine = jnp.cos(angles), jnp.sin(angles)
+    cosine = jnp.concatenate([cosine, cosine], axis=1)
+    sine = jnp.concatenate([-sine, sine], axis=1)
+    table = pl.BlockSpec((seq_len, HEAD_WIDTH), lambda g: (0, 0))
+    return pl.pallas_call(
+        functools.partial(attend_kernel, group),
+        grid=(local_kv,),
+        out_shape=jax.ShapeDtypeStruct((seq_len, part_query), jnp.bfloat16),
+        in_specs=[
+            pl.BlockSpec((seq_len, group * HEAD_WIDTH), lambda g: (0, g)),
+            pl.BlockSpec((seq_len, HEAD_WIDTH), lambda g: (0, key_at + g)),
+            pl.BlockSpec((seq_len, HEAD_WIDTH), lambda g: (0, key_at + local_kv + g)),
+            table,
+            table,
+        ],
+        out_specs=pl.BlockSpec((seq_len, group * HEAD_WIDTH), lambda g: (0, g)),
+        compiler_params=pltpu.CompilerParams(vmem_limit_bytes=24 << 20),
+    )(product, product, product, cosine, sine)
 
 
 def per_device(
@@ -270,12 +424,8 @@
         proj,
         preferred_element_type=jnp.float32,
     ).astype(jnp.bfloat16)
-    partial = partial.reshape(outer, inner, token_count, part_model).transpose(1, 0, 2, 3)
-    partial = sum_blocks(
-        partial.reshape(inner, outer * token_count, part_model), inner, True, 1, jnp.bfloat16
-    )
-    image_cols = sum_blocks(
-        partial.reshape(outer, token_count, part_model), inner, False, 2, jnp.bfloat16
+    image_cols = reduce_blocks(
+        partial.reshape(outer, inner, token_count, part_model), 1
     ).reshape(tile_rows, tile_tok, part_model)
 
     empty_slots = jnp.zeros((data_count, slot_count) + image_cols.shape[1:], jnp.bfloat16)
@@ -302,16 +452,11 @@
     normalized = normalized.reshape(seq_len, held_rows, inner, depth).transpose(2, 0, 1, 3)
     normalized = exchange(
         normalized.reshape(inner, seq_len, held_rows * depth), inner, True, 4
-    ).reshape(inner * seq_len, held_rows * depth)
-    product = 0.0
-    for step, piece in enumerate(tensor_pieces(normalized)):
-        start = (tensor_index - step) % tensor_count * (held_rows * depth)
-        rows = lax.dynamic_slice_in_dim(weight, start, held_rows * depth, 0)
-        product = product + jnp.dot(piece, rows, preferred_element_type=jnp.float32)
-    product = product.astype(jnp.bfloat16).reshape(inner, seq_len, -1)
-    product = sum_blocks(product, inner, True, 5, jnp.float32)
+    )
+    pieces = tensor_pieces(normalized)
+    product = product_blocks(pieces, weight, 5)
     part_query = w_query.shape[1]
-    context = attend(product[:, :part_query], product[:, part_query:].reshape(seq_len, 2, -1))
+    context = attend(product, part_query)
     return context.reshape(1, seq_len, context.shape[1])
 
 

time: 596 us -> 522 us (0.88)
  matrix products: 48.6 us -> 6.69 us
  local copies, waits for them, and re-layouts: 93.5 us -> 57.2 us
  other arithmetic: 21.4 us -> 12.9 us
  Pallas kernels: 408 us -> 416 us
    dot_general x4 -> x0, matrix products: 39.9 us -> none  [the longest x2 33.7 us: per_device(): product = product + jnp.dot(piece, rows, preferred_element_type=jnp.float32)]
    pallas_call x3, Pallas kernels: 118 us -> 147 us  [exchange(): pl.pallas_call(functools.partial(exchange_kernel, size, inner, plane), ou...]
    pallas_call x3, Pallas kernels: 290 us -> 269 us  [the longest x1 139 us: reduce_blocks(): pl.pallas_call(functools.partial(reduce_kernel, inner, chunks, math.gcd(t...]
    slice x5 -> x0, local copies, waits for them, and re-layouts: 12.2 us -> none  [the longest x2 6 us: attend(): key_value_complete[:, 1].reshape(seq_len, local_kv, HEAD_WIDTH)]
    reshape x2 -> x0, local copies, waits for them, and re-layouts: 11.4 us -> none  [the longest x1 7.74 us: per_device(): partial.reshape(outer, inner, token_count, part_model).transpose(1, 0, 2, 3)]
    unnamed x30 -> x23, local copies, waits for them, and re-layouts: 23.7 us -> 13.9 us
  transfers between devices with their start and end apart: 3 -> 3, of which waited for: 0 -> 1; matrix products, arithmetic and copies ran while one was open for 16% -> 13% of each run, Pallas kernels for 51% -> 55%
where the time goes in v2:
time: 522 us; the launch traced here: 516 us
  Pallas kernels  416 us (80%)
  local copies, waits for them, and re-layouts  57.2 us (11%)
  between operations  14.3 us (3%)
  other arithmetic  12.9 us (2%)
  matrix products  6.69 us (1%)
    pallas_call x3, Pallas kernels, exchange(): pl.pallas_call(functools.partial(exchange_kernel, size, inner, plane), ou...  147 us
    pallas_call x1, Pallas kernels, reduce_blocks(): pl.pallas_call(functools.partial(reduce_kernel, inner, chunks, math.gcd(t...  139 us
    pallas_call x1, Pallas kernels, product_blocks(): pl.pallas_call(functools.partial(product_kernel, inner, count, math.gcd(c...  121 us
    unnamed x23, local copies, waits for them, and re-layouts  13.9 us
    dynamic_update_slice x2, local copies, waits for them, and re-layouts, per_device(): whole = lax.dynamic_update_slice_in_dim(whole, piece, start, 2)  13.1 us
  transfers between devices with their start and end apart: 3, of which 1 were waited for; matrix products, arithmetic and copies ran while one was open for 13% of the time, Pallas kernels for 55%

profile of v2, /device:TPU:13, one launch (start us, length us, event | category | flops | bytes accessed | tf_op | source)
XLA Modules:
  0.0 516.1 jit_solution(9623340698188769713)
XLA Ops:
  6.5 4.1 copy.34
  10.6 0.2 copy.25
  10.9 1.9 pad_maximum_fusion
  12.8 2.0 copy.20
  14.8 0.7 collective-permute-start
  15.5 3.9 copy.23
  19.4 0.1 copy.19
  19.5 0.1 reduce
  20.3 0.7 fusion.17
  20.9 0.6 iota_compare_fusion.1
  21.5 0.1 broadcast_in_dim.34
  21.6 0.1 broadcast_in_dim.35
  21.7 6.9 %dynamic_update_slice.9 = bf16[64,2,3200]{2,0,1:T(8,128)(2,1)S(1)} dynamic-update-slice(bf16[64,2,3200]{2,0,1:T(8,128)(2,1)S(1)} %broadcast_in_dim.60, bf16[64,2,1600]{2,0,1:T(8,128)(2,1)} %copy.20, s32[]{:T(128)} %constant.85.clone.1, s32[]{:T(128)} %constant.85.clone.1, s32[]{:T(128)S(6)} %select_n.122) | dynamic-update-slice | bytes 819204 | tf_op jit(solution)/shard_map/dynamic_update_slice | solution.py:415
  28.7 0.2 convert_reduce_fusion.1
  28.9 0.6 fusion.15
  29.6 0.2 select_reduce_fusion
  29.8 6.2 %dynamic_update_slice.10 = bf16[64,2,3200]{2,0,1:T(8,128)(2,1)S(1)} dynamic-update-slice(bf16[64,2,3200]{2,0,1:T(8,128)(2,1)S(1)} %dynamic_update_slice.9, bf16[64,2,1600]{2,0,1:T(8,128)(2,1)} %collective-permute-done, s32[]{:T(128)} %constant.85.clone.1, s32[]{:T(128)} %constant.85.clone.1, s32[]{:T(128)S(6)} %select_n.124) | dynamic-update-slice | bytes 819204 | tf_op jit(solution)/shard_map/dynamic_update_slice | solution.py:415
  35.9 0.2 convert_reduce_fusion
  36.2 0.4 fusion.5
  36.6 0.4 fusion.8
  37.0 3.1 reshape.269
  40.1 1.1 copy.22
  41.2 0.6 reshape.270.x_ref
  41.9 52.8 %shard_map.100 = bf16[16,64,400]{2,1,0:T(8,128)(2,1)S(1)} custom-call(bf16[16,64,400]{2,1,0:T(8,128)(2,1)S(1)} %reshape.270.x_ref), custom_call_target="tpu_custom_call" | custom-call | bytes 16384000 | tf_op jit(solution)/shard_map/pallas_call | solution.py:282
  94.6 6.7 %convolution_convert_fusion = bf16[1024,4096]{1,0:T(8,128)(2,1)S(1)} fusion(bf16[1024,400]{1,0:T(8,128)(2,1)S(1)} %bitcast.46, bf16[400,4096]{1,0:T(8,128)(2,1)} %bitcast.51), kind=kOutput, calls=%fused_computation.4 | convolution fusion | flops 3359637504 | bytes 12484608 | tf_op jit(solution)/shard_map/dot_general | solution.py:422
  101.3 139.3 %shard_map.101 = bf16[64,4096]{1,0:T(8,128)(2,1)S(1)} custom-call(bf16[4,4,64,4096]{3,2,1,0:T(8,128)(2,1)S(1)} %bitcast.43), custom_call_target="tpu_custom_call" | custom-call | bytes 251658240 | tf_op jit(solution)/shard_map/pallas_call | solution.py:168
  240.6 0.1 broadcast.300
  240.8 0.8 scatter_fusion
  241.5 54.8 %shard_map.102 = bf16[16,1,8,4096]{3,2,1,0:T(8,128)(2,1)S(1)} custom-call(bf16[16,1,8,4096]{3,2,1,0:T(8,128)(2,1)S(1)} %bitcast.44), custom_call_target="tpu_custom_call" | custom-call | bytes 20971520 | tf_op jit(solution)/shard_map/pallas_call | solution.py:282
  296.4 1.6 gather_fusion
  298.0 3.2 bitcast_select_fusion
  301.2 7.1 %dynamic_update_slice.11 = bf16[384,4096]{1,0:T(8,128)(2,1)S(1)} dynamic-update-slice(bf16[384,4096]{1,0:T(8,128)(2,1)S(1)} %bitcast.47, bf16[128,4096]{1,0:T(8,128)(2,1)} %bitcast_select_fusion, s32[]{:T(128)S(6)} %select_n.130, s32[]{:T(128)} %constant.85.clone.1) | dynamic-update-slice | bytes 2097156 | tf_op jit(solution)/shard_map/dynamic_update_slice | solution.py:441
  308.3 0.7 fusion
  309.0 3.0 psum.7
  312.0 2.7 fusion.2
  314.7 4.8 reshape.276
  319.5 4.1 copy.27
  323.6 4.7 reshape.277.x_ref
  328.3 39.4 %shard_map.103.refs_0_ = bf16[4,384,1024]{2,1,0:T(8,128)(2,1)S(1)} custom-call(bf16[4,384,1024]{2,1,0:T(8,128)(2,1)S(1)} %reshape.277.x_ref), custom_call_target="tpu_custom_call" | custom-call | bytes 62914560 | tf_op jit(solution)/shard_map/pallas_call | solution.py:282
  367.7 1.7 copy-done.1
  369.3 0.5 collective-permute-start.1
  369.8 0.7 fusion.11
  370.6 0.2 pad_maximum_fusion.1
  370.8 4.3 collective-permute-done.1.refs_1_
  375.1 1.7 copy-done.9
  376.8 121.2 %shard_map.104.q_ref.k_ref.v_ref = f32[384,3072]{1,0:T(8,128)} custom-call(bf16[4,384,1024]{2,1,0:T(8,128)(2,1)} %copy-done.1, bf16[4,384,1024]{2,1,0:T(8,128)(2,1)} %copy-done.9, bf16[2048,3072]{1,0:T(8,128)(2,1)} %all-gather.2.cloned.1.call-done.refs_2_), custom_call_target="tpu_custom_call" | custom-call | flops 19327352832 | bytes 209715200 | tf_op jit(solution)/shard_map/pallas_call | solution.py:256
  498.0 2.3 copy-done
  500.3 8.9 %shard_map.105 = bf16[384,2048]{1,0:T(8,128)(2,1)} custom-call(f32[384,3072]{1,0:T(8,128)S(1)} %copy-done, f32[384,3072]{1,0:T(8,128)S(1)} %copy-done, f32[384,3072]{1,0:T(8,128)S(1)} %copy-done, f32[384,128]{1,0:T(8,128)S(1)} %get-tuple-element.11.cos_ref, f32[384,128]{1,0:T(8,128)S(1)} %get-tuple-element.12.sin_ref), custom_call_target="tpu_custom_call" | custom-call | tf_op jit(solution)/shard_map/pallas_call | solution.py:349
  (31 shorter events, 0.2 us)
Async XLA Ops:
  6.5 4.3 copy-start.4
  6.5 4.1 copy-start.5
  6.5 368.6 %all-gather.2.cloned.1.call-start = ((), (), s32[]{:S(2)}) async-start(), calls=%async_computation | async-start | bytes 15728640 | tf_op jit(solution)/shard_map/all_gather | solution.py:390
  12.8 2.7 copy-start.3
  14.8 15.0 %collective-permute-start = (bf16[64,2,1600]{2,0,1:T(8,128)(2,1)}, bf16[64,2,1600]{2,0,1:T(8,128)(2,1)}, u32[]{:S(2)}, u32[]{:S(2)}) collective-permute-start(bf16[64,2,1600]{2,0,1:T(8,128)(2,1)} %copy.20), channel_id=1, source_target_pairs={{0,1},{1,0},{2,3},{3,2},{4,5},{5,4},{6,7},{7,6},{8,9},{9,8},{10,11... | collective-permute-start | bytes 1228808 | tf_op jit(solution)/shard_map/ppermute | solution.py:306
  15.5 3.9 copy-start.8
  19.4 17.2 %copy-start.6 = (f32[2,3200]{1,0:T(2,128)S(1)}, f32[2,3200]{1,0:T(2,128)}, u32[]{:S(2)}) copy-start(f32[2,3200]{1,0:T(2,128)} %param.12) | copy-start | bytes 76804
  19.4 17.2 %copy-start.7 = (f32[2,3200]{1,0:T(2,128)S(1)}, f32[2,3200]{1,0:T(2,128)}, u32[]{:S(2)}) copy-start(f32[2,3200]{1,0:T(2,128)} %param.11) | copy-start | bytes 76804
  298.0 3.2 copy-start.2
  301.2 10.8 %dynamic-slice-start = ((f32[8192]{0:T(1024)}, s32[]{:T(128)}), f32[4096]{0:T(1024)S(1)}, s32[]{:S(2)}) async-start(f32[8192]{0:T(1024)} %param.15, s32[]{:T(128)} %select_n.132), calls=%async_computation.1 | async-start | bytes 33280 | tf_op jit(solution)/shard_map/dynamic_slice | solution.py:447
  367.7 1.7 copy-start.1
  369.3 5.8 %collective-permute-start.1 = (bf16[4,384,1024]{2,1,0:T(8,128)(2,1)S(1)}, bf16[4,384,1024]{2,1,0:T(8,128)(2,1)S(1)}, u32[]{:S(2)}, u32[]{:S(2)}) collective-permute-start(bf16[4,384,1024]{2,1,0:T(8,128)(2,1)S(1)} %shard_map.103.refs_0_), channel_id=1, source_target_pairs={{0,1},{1,0},{2,3},{3,2},{4,5},{5,4},{6,7},{7,6},{8,9},{9,8},{10,11... | collective-permute-start | bytes 9437192 | tf_op jit(solution)/shard_map/ppermute | solution.py:306
  375.1 1.7 copy-start.9
  498.0 2.3 copy-start
Sparse Core Ops, SparseCore 0:
  12.9 305.1 all-gather.1
